TPU v7x, 32 devices: a whole 2x2x4 slice. The times are simulated.
32 devices in a mesh: tm: 16 (over z, y, core), space: 2 (over x).
Axes of the slice: x: 2, y: 2, z: 4, core: 2. Of those that a mesh axis runs over, the one named last changes fastest.
Arguments:
- control: float32 [32, 512], P('space'), may hold values from -0.6 to 0.6
- initial: float32 [32, 512], P('space'), may hold values from -6 to 6
- diffusion: float32 [32, 512], P('space'), may hold values from 0.1 to 1
- reaction: float32 [32, 512], P('space'), may hold values from 7.8125e-05 to 0.1
- forward_guess: float32 [16, 32, 512], P('tm', 'space'), may hold values from -1.5 to 1.5
- adjoint_guess: float32 [16, 32, 512], P('tm', 'space'), may hold values from -1.5 to 1.5
- observed: float32 [16, 32, 512], P('tm', 'space'), may hold values from -6 to 6
Outputs:
- forward_states: float32 [16, 32, 512], P('tm', 'space')
- adjoint_states: float32 [16, 32, 512], P('tm', 'space')
- control_gradient: float32 [32, 512], P('space')
All inputs are finite; a program needn't handle non-finite values.
Results may differ from a plain program's by a relative error of at most 0.00015.
Values sent between devices are 32-bit elements; how exact they have to be, the bound alone decides.
A program may use at most 128 MiB of HBM per device.

v0:
```python
import jax
import jax.numpy as jnp
from jax import lax
from jax.sharding import PartitionSpec as P

SWEEPS = 3
COARSEN = 8


def with_halo(value, sides, width):
    for axis, dim in sides:
        size, length = (lax.axis_size(axis), value.shape[dim])
        up = [(i, (i + 1) % size) for i in range(size - 1)]
        down = [(j, i) for i, j in up]
        last = lax.slice_in_dim(value, length - width, length, axis=dim)
        leading = lax.slice_in_dim(value, 0, width, axis=dim)
        before = lax.ppermute(last, axis, up)
        after = lax.ppermute(leading, axis, down)
        value = jnp.concatenate([before, value, after], axis=dim)
    return value


def passed_along(block, axis, distance):
    devices = range(lax.axis_size(axis))
    route = [(i - distance, i) for i in devices if i - distance in devices]
    return lax.ppermute(block, axis, route)


def neighbours(source):
    zero_row = jnp.zeros_like(source[..., :1, :])
    zero_column = jnp.zeros_like(source[..., :, :1])
    vertical = jnp.concatenate([source[..., 1:, :], zero_row], -2) + jnp.concatenate(
        [zero_row, source[..., :-1, :]], -2
    )
    lateral = jnp.concatenate([source[..., :, 1:], zero_column], -1) + jnp.concatenate(
        [zero_column, source[..., :, :-1]], -1
    )
    return vertical + lateral


def forward_step(previous, control, spread, diagonal):
    padded = with_halo(previous + control, (("space", 0),), SWEEPS)
    iterate = padded
    for number in range(SWEEPS):
        iterate = (padded + spread * neighbours(iterate)) / diagonal
    return iterate[SWEEPS : SWEEPS + previous.shape[0]]


def adjoint_step(following, misfit, weight, diagonal):
    padded = with_halo(following + misfit, (("space", 0),), SWEEPS)
    carried = padded
    summed = padded
    for number in range(SWEEPS - 1):
        carried = neighbours(weight * carried)
        summed = summed + carried
    result = summed / diagonal + neighbours(weight * carried)
    return result[SWEEPS : SWEEPS + following.shape[0]]


def entries(own_forward, own_adjoint, initial):
    arriving = passed_along(own_forward, "tm", 1)
    entry_forward = jnp.where(lax.axis_index("tm") == 0, initial, arriving)
    entry_adjoint = passed_along(own_adjoint, "tm", -1)
    return (entry_forward, entry_adjoint)


def relax(own_forward, own_adjoint, initial, control, target, spread, weight, diagonal, first_pass):
    entry_forward, entry_adjoint = entries(own_forward, own_adjoint, initial)
    states = []
    current = entry_forward
    for number in range(COARSEN - 1):
        current = forward_step(current, control, spread, diagonal)
        states.append(current)
    points = states + [own_forward]
    current = entry_adjoint
    fine_total = jnp.zeros_like(own_adjoint)
    for position in range(COARSEN, 1, -1):
        misfit = (points[position - 1] - target) / COARSEN
        current = adjoint_step(current, misfit, weight, diagonal)
        fine_total = fine_total + current
    if first_pass:
        forward_residual = forward_step(states[-1], control, spread, diagonal) - own_forward
        adjoint_residual = (
            adjoint_step(current, (points[0] - target) / COARSEN, weight, diagonal) - own_adjoint
        )
        return (forward_residual, adjoint_residual)
    return fine_total


def shards(control, initial, diffusion, reaction, forward_guess, adjoint_guess, observed):
    coefficients = with_halo(jnp.stack((diffusion, reaction)), (("space", 1),), SWEEPS)
    spread = coefficients[0]
    diagonal = 1.0 + 4.0 * spread + coefficients[1]
    weight = spread / diagonal
    own_forward = forward_guess[0]
    own_adjoint = adjoint_guess[0]
    target = observed[0]
    forward_residual, adjoint_residual = relax(
        own_forward, own_adjoint, initial, control, target, spread, weight, diagonal, True
    )
    damping = 1.0 / (1.0 + COARSEN * reaction)
    forward_correction = forward_residual
    adjoint_correction = adjoint_residual
    damping_power = damping
    section_count = (lax.axis_size("tm") - 1).bit_length()
    for section_index in range(section_count):
        distance = 1 << section_index
        from_lower = passed_along(forward_correction, "tm", distance)
        from_upper = passed_along(adjoint_correction, "tm", -distance)
        forward_correction = forward_correction + damping_power * from_lower
        adjoint_correction = adjoint_correction + damping_power * from_upper
        damping_power = damping_power * damping_power
    forward_states = own_forward + forward_correction
    adjoint_states = own_adjoint + adjoint_correction
    steps_total = COARSEN * lax.axis_size("tm")
    fine_local = relax(
        forward_states, adjoint_states, initial, control, target, spread, weight, diagonal, False
    )
    gradient = lax.psum(adjoint_states + fine_local, "tm") / steps_total
    return (forward_states[None], adjoint_states[None], gradient)


def solution(mesh):
    return jax.shard_map(
        shards,
        mesh=mesh,
        in_specs=(
            P("space", None),
            P("space", None),
            P("space", None),
            P("space", None),
            P("tm", "space", None),
            P("tm", "space", None),
            P("tm", "space", None),
        ),
        out_specs=(P("tm", "space", None), P("tm", "space", None), P("space", None)),
        check_vma=False,
    )
```

profile of v0, /device:TPU:0, one launch (start us, length us, event | category | flops | bytes accessed | tf_op | source)
XLA Modules:
  0.0 339.3 jit_solution(6329233354328219785)
XLA Ops:
  2.8 4.9 %collective-permute-start.3 = (f32[2,3,512]{2,1,0:T(4,128)S(1)}, f32[2,3,512]{2,1,0:T(4,128)S(1)}, u32[]{:S(2)}, u32[]{:S(2)}) collective-permute-start(f32[2,3,512]{2,1,0:T(4,128)S(1)} %get-tuple-element.104), channel_id=1, source_target_pairs={{0,1},{2,3},{4,5},{6,7},{8,9},{10,11},{12,13},{14,15},{16,17},{18,... | collective-permute-start | bytes 36872 | tf_op jit(solution)/shard_map/ppermute | solution.py:17
  14.9 4.5 %collective-permute-start.24 = (f32[3,512]{1,0:T(4,128)S(1)}, f32[3,512]{1,0:T(4,128)S(1)}, u32[]{:S(2)}, u32[]{:S(2)}) collective-permute-start(f32[3,512]{1,0:T(4,128)S(1)} %get-tuple-element.557), channel_id=1, source_target_pairs={{0,1},{2,3},{4,5},{6,7},{8,9},{10,11},{12,13},{14,15},{16,17},{18,... | collective-permute-start | bytes 18440 | tf_op jit(solution)/shard_map/ppermute | solution.py:17
  20.8 4.5 %collective-permute-start.1 = (f32[3,512]{1,0:T(4,128)S(1)}, f32[3,512]{1,0:T(4,128)S(1)}, u32[]{:S(2)}, u32[]{:S(2)}) collective-permute-start(f32[3,512]{1,0:T(4,128)S(1)} %get-tuple-element.555), channel_id=1, source_target_pairs={{0,1},{2,3},{4,5},{6,7},{8,9},{10,11},{12,13},{14,15},{16,17},{18,... | collective-permute-start | bytes 18440 | tf_op jit(solution)/shard_map/ppermute | solution.py:17
  28.6 4.5 %collective-permute-start.5 = (f32[3,512]{1,0:T(4,128)S(1)}, f32[3,512]{1,0:T(4,128)S(1)}, u32[]{:S(2)}, u32[]{:S(2)}) collective-permute-start(f32[3,512]{1,0:T(4,128)S(1)} %get-tuple-element.553), channel_id=1, source_target_pairs={{0,1},{2,3},{4,5},{6,7},{8,9},{10,11},{12,13},{14,15},{16,17},{18,... | collective-permute-start | bytes 18440 | tf_op jit(solution)/shard_map/ppermute | solution.py:17
  36.4 4.5 %collective-permute-start.7 = (f32[3,512]{1,0:T(4,128)S(1)}, f32[3,512]{1,0:T(4,128)S(1)}, u32[]{:S(2)}, u32[]{:S(2)}) collective-permute-start(f32[3,512]{1,0:T(4,128)S(1)} %get-tuple-element.551), channel_id=1, source_target_pairs={{0,1},{2,3},{4,5},{6,7},{8,9},{10,11},{12,13},{14,15},{16,17},{18,... | collective-permute-start | bytes 18440 | tf_op jit(solution)/shard_map/ppermute | solution.py:17
  44.2 4.5 %collective-permute-start.9 = (f32[3,512]{1,0:T(4,128)S(1)}, f32[3,512]{1,0:T(4,128)S(1)}, u32[]{:S(2)}, u32[]{:S(2)}) collective-permute-start(f32[3,512]{1,0:T(4,128)S(1)} %get-tuple-element.549), channel_id=1, source_target_pairs={{0,1},{2,3},{4,5},{6,7},{8,9},{10,11},{12,13},{14,15},{16,17},{18,... | collective-permute-start | bytes 18440 | tf_op jit(solution)/shard_map/ppermute | solution.py:17
  52.0 4.5 %collective-permute-start.11 = (f32[3,512]{1,0:T(4,128)S(1)}, f32[3,512]{1,0:T(4,128)S(1)}, u32[]{:S(2)}, u32[]{:S(2)}) collective-permute-start(f32[3,512]{1,0:T(4,128)S(1)} %get-tuple-element.547), channel_id=1, source_target_pairs={{0,1},{2,3},{4,5},{6,7},{8,9},{10,11},{12,13},{14,15},{16,17},{18,... | collective-permute-start | bytes 18440 | tf_op jit(solution)/shard_map/ppermute | solution.py:17
  59.8 4.5 %collective-permute-start.13 = (f32[3,512]{1,0:T(4,128)S(1)}, f32[3,512]{1,0:T(4,128)S(1)}, u32[]{:S(2)}, u32[]{:S(2)}) collective-permute-start(f32[3,512]{1,0:T(4,128)S(1)} %get-tuple-element.545), channel_id=1, source_target_pairs={{0,1},{2,3},{4,5},{6,7},{8,9},{10,11},{12,13},{14,15},{16,17},{18,... | collective-permute-start | bytes 18440 | tf_op jit(solution)/shard_map/ppermute | solution.py:17
  67.6 4.5 %collective-permute-start.15 = (f32[3,512]{1,0:T(4,128)S(1)}, f32[3,512]{1,0:T(4,128)S(1)}, u32[]{:S(2)}, u32[]{:S(2)}) collective-permute-start(f32[3,512]{1,0:T(4,128)S(1)} %get-tuple-element.543), channel_id=1, source_target_pairs={{0,1},{2,3},{4,5},{6,7},{8,9},{10,11},{12,13},{14,15},{16,17},{18,... | collective-permute-start | bytes 18440 | tf_op jit(solution)/shard_map/ppermute | solution.py:17
  75.4 4.5 %collective-permute-start.17 = (f32[3,512]{1,0:T(4,128)S(1)}, f32[3,512]{1,0:T(4,128)S(1)}, u32[]{:S(2)}, u32[]{:S(2)}) collective-permute-start(f32[3,512]{1,0:T(4,128)S(1)} %get-tuple-element.527), channel_id=1, source_target_pairs={{0,1},{2,3},{4,5},{6,7},{8,9},{10,11},{12,13},{14,15},{16,17},{18,... | collective-permute-start | bytes 18440 | tf_op jit(solution)/shard_map/ppermute | solution.py:17
  81.2 4.5 %collective-permute-start.26 = (f32[3,512]{1,0:T(4,128)S(1)}, f32[3,512]{1,0:T(4,128)S(1)}, u32[]{:S(2)}, u32[]{:S(2)}) collective-permute-start(f32[3,512]{1,0:T(4,128)S(1)} %get-tuple-element.541), channel_id=1, source_target_pairs={{0,1},{2,3},{4,5},{6,7},{8,9},{10,11},{12,13},{14,15},{16,17},{18,... | collective-permute-start | bytes 18440 | tf_op jit(solution)/shard_map/ppermute | solution.py:17
  89.0 4.5 %collective-permute-start.28 = (f32[3,512]{1,0:T(4,128)S(1)}, f32[3,512]{1,0:T(4,128)S(1)}, u32[]{:S(2)}, u32[]{:S(2)}) collective-permute-start(f32[3,512]{1,0:T(4,128)S(1)} %get-tuple-element.539), channel_id=1, source_target_pairs={{0,1},{2,3},{4,5},{6,7},{8,9},{10,11},{12,13},{14,15},{16,17},{18,... | collective-permute-start | bytes 18440 | tf_op jit(solution)/shard_map/ppermute | solution.py:17
  96.8 4.5 %collective-permute-start.30 = (f32[3,512]{1,0:T(4,128)S(1)}, f32[3,512]{1,0:T(4,128)S(1)}, u32[]{:S(2)}, u32[]{:S(2)}) collective-permute-start(f32[3,512]{1,0:T(4,128)S(1)} %get-tuple-element.537), channel_id=1, source_target_pairs={{0,1},{2,3},{4,5},{6,7},{8,9},{10,11},{12,13},{14,15},{16,17},{18,... | collective-permute-start | bytes 18440 | tf_op jit(solution)/shard_map/ppermute | solution.py:17
  132.5 5.2 %collective-permute-start.20 = (f32[16,512]{1,0:T(8,128)S(1)}, f32[16,512]{1,0:T(8,128)S(1)}, u32[]{:S(2)}, u32[]{:S(2)}) collective-permute-start(f32[16,512]{1,0:T(8,128)S(1)} %multiply_add_fusion.5), channel_id=1, source_target_pairs={{0,4},{2,6},{4,8},{6,10},{8,12},{10,14},{12,16},{14,18},{16,20},{1... | collective-permute-start | bytes 98312 | tf_op jit(solution)/shard_map/ppermute | solution.py:26
  139.7 5.9 %collective-permute-start.21 = (f32[16,512]{1,0:T(8,128)S(1)}, f32[16,512]{1,0:T(8,128)S(1)}, u32[]{:S(2)}, u32[]{:S(2)}) collective-permute-start(f32[16,512]{1,0:T(8,128)S(1)} %multiply_add_fusion.4), channel_id=1, source_target_pairs={{0,8},{2,10},{4,12},{6,14},{8,16},{10,18},{12,20},{14,22},{16,24},... | collective-permute-start | bytes 98312 | tf_op jit(solution)/shard_map/ppermute | solution.py:26
  154.3 4.8 %collective-permute-done.42 = f32[16,512]{1,0:T(8,128)S(1)} collective-permute-done((f32[16,512]{1,0:T(8,128)S(1)}, f32[16,512]{1,0:T(8,128)S(1)}, u32[]{:S(2)}, u32[]{:S(2)}) %collective-permute-start.42) | collective-permute-done | bytes 32800 | tf_op jit(solution)/shard_map/ppermute | solution.py:26
  160.4 5.4 %collective-permute-start.22 = (f32[16,512]{1,0:T(8,128)S(1)}, f32[16,512]{1,0:T(8,128)S(1)}, u32[]{:S(2)}, u32[]{:S(2)}) collective-permute-start(f32[16,512]{1,0:T(8,128)S(1)} %get-tuple-element.525), channel_id=1, source_target_pairs={{0,16},{2,18},{4,20},{6,22},{8,24},{10,26},{12,28},{14,30},{1,17},... | collective-permute-start | bytes 98312 | tf_op jit(solution)/shard_map/ppermute | solution.py:26
  170.4 4.5 %collective-permute-start.45 = (f32[3,512]{1,0:T(4,128)S(1)}, f32[3,512]{1,0:T(4,128)S(1)}, u32[]{:S(2)}, u32[]{:S(2)}) collective-permute-start(f32[3,512]{1,0:T(4,128)S(1)} %get-tuple-element.509), channel_id=1, source_target_pairs={{0,1},{2,3},{4,5},{6,7},{8,9},{10,11},{12,13},{14,15},{16,17},{18,... | collective-permute-start | bytes 18440 | tf_op jit(solution)/shard_map/ppermute | solution.py:17
  180.5 4.5 %collective-permute-start.48 = (f32[3,512]{1,0:T(4,128)S(1)}, f32[3,512]{1,0:T(4,128)S(1)}, u32[]{:S(2)}, u32[]{:S(2)}) collective-permute-start(f32[3,512]{1,0:T(4,128)S(1)} %get-tuple-element.523), channel_id=1, source_target_pairs={{0,1},{2,3},{4,5},{6,7},{8,9},{10,11},{12,13},{14,15},{16,17},{18,... | collective-permute-start | bytes 18440 | tf_op jit(solution)/shard_map/ppermute | solution.py:17
  219.4 4.5 %collective-permute-start.58 = (f32[3,512]{1,0:T(4,128)S(1)}, f32[3,512]{1,0:T(4,128)S(1)}, u32[]{:S(2)}, u32[]{:S(2)}) collective-permute-start(f32[3,512]{1,0:T(4,128)S(1)} %get-tuple-element.513), channel_id=1, source_target_pairs={{0,1},{2,3},{4,5},{6,7},{8,9},{10,11},{12,13},{14,15},{16,17},{18,... | collective-permute-start | bytes 18440 | tf_op jit(solution)/shard_map/ppermute | solution.py:17
  235.0 4.5 %collective-permute-start.62 = (f32[3,512]{1,0:T(4,128)S(1)}, f32[3,512]{1,0:T(4,128)S(1)}, u32[]{:S(2)}, u32[]{:S(2)}) collective-permute-start(f32[3,512]{1,0:T(4,128)S(1)} %get-tuple-element.507), channel_id=1, source_target_pairs={{0,1},{2,3},{4,5},{6,7},{8,9},{10,11},{12,13},{14,15},{16,17},{18,... | collective-permute-start | bytes 18440 | tf_op jit(solution)/shard_map/ppermute | solution.py:17
  250.6 4.5 %collective-permute-start.66 = (f32[3,512]{1,0:T(4,128)S(1)}, f32[3,512]{1,0:T(4,128)S(1)}, u32[]{:S(2)}, u32[]{:S(2)}) collective-permute-start(f32[3,512]{1,0:T(4,128)S(1)} %get-tuple-element.503), channel_id=1, source_target_pairs={{0,1},{2,3},{4,5},{6,7},{8,9},{10,11},{12,13},{14,15},{16,17},{18,... | collective-permute-start | bytes 18440 | tf_op jit(solution)/shard_map/ppermute | solution.py:17
  266.2 4.5 %collective-permute-start.70 = (f32[3,512]{1,0:T(4,128)S(1)}, f32[3,512]{1,0:T(4,128)S(1)}, u32[]{:S(2)}, u32[]{:S(2)}) collective-permute-start(f32[3,512]{1,0:T(4,128)S(1)} %get-tuple-element.499), channel_id=1, source_target_pairs={{0,1},{2,3},{4,5},{6,7},{8,9},{10,11},{12,13},{14,15},{16,17},{18,... | collective-permute-start | bytes 18440 | tf_op jit(solution)/shard_map/ppermute | solution.py:17
  280.4 58.3 %psum.7 = f32[16,512]{1,0:T(8,128)S(1)} all-reduce(f32[16,512]{1,0:T(8,128)S(1)} %fusion.4), channel_id=1, replica_groups=mesh['tm'=16,'space'=2] {'tm'}, use_global_device_ids=true, to_apply=%region_0.1 | all-reduce | flops 8192 | bytes 65536 | tf_op jit(solution)/shard_map/psum | solution.py:119
  (483 shorter events, 169.9 us)
Async XLA Ops:
  1.5 10.5 %collective-permute-start.4 = (f32[2,3,512]{2,1,0:T(4,128)S(1)}, f32[2,3,512]{2,1,0:T(4,128)S(1)}, u32[]{:S(2)}, u32[]{:S(2)}) collective-permute-start(f32[2,3,512]{2,1,0:T(4,128)S(1)} %get-tuple-element.105), channel_id=1, source_target_pairs={{1,0},{3,2},{5,4},{7,6},{9,8},{11,10},{13,12},{15,14},{17,16},{19,... | collective-permute-start | bytes 36872 | tf_op jit(solution)/shard_map/ppermute | solution.py:18
  2.8 9.3 %collective-permute-start.3 = (f32[2,3,512]{2,1,0:T(4,128)S(1)}, f32[2,3,512]{2,1,0:T(4,128)S(1)}, u32[]{:S(2)}, u32[]{:S(2)}) collective-permute-start(f32[2,3,512]{2,1,0:T(4,128)S(1)} %get-tuple-element.104), channel_id=1, source_target_pairs={{0,1},{2,3},{4,5},{6,7},{8,9},{10,11},{12,13},{14,15},{16,17},{18,... | collective-permute-start | bytes 36872 | tf_op jit(solution)/shard_map/ppermute | solution.py:17
  9.0 10.5 %collective-permute-start = (f32[16,512]{1,0:T(8,128)S(1)}, f32[16,512]{1,0:T(8,128)S(1)}, u32[]{:S(2)}, u32[]{:S(2)}) collective-permute-start(f32[16,512]{1,0:T(8,128)S(1)} %bitcast.159), channel_id=1, source_target_pairs={{0,2},{2,4},{4,6},{6,8},{8,10},{10,12},{12,14},{14,16},{16,18},{18... | collective-permute-start | bytes 98312 | tf_op jit(solution)/shard_map/ppermute | solution.py:26
  13.6 11.8 %collective-permute-start.25 = (f32[3,512]{1,0:T(4,128)S(1)}, f32[3,512]{1,0:T(4,128)S(1)}, u32[]{:S(2)}, u32[]{:S(2)}) collective-permute-start(f32[3,512]{1,0:T(4,128)S(1)} %get-tuple-element.558), channel_id=1, source_target_pairs={{1,0},{3,2},{5,4},{7,6},{9,8},{11,10},{13,12},{15,14},{17,16},{19,... | collective-permute-start | bytes 18440 | tf_op jit(solution)/shard_map/ppermute | solution.py:18
  14.9 10.5 %collective-permute-start.24 = (f32[3,512]{1,0:T(4,128)S(1)}, f32[3,512]{1,0:T(4,128)S(1)}, u32[]{:S(2)}, u32[]{:S(2)}) collective-permute-start(f32[3,512]{1,0:T(4,128)S(1)} %get-tuple-element.557), channel_id=1, source_target_pairs={{0,1},{2,3},{4,5},{6,7},{8,9},{10,11},{12,13},{14,15},{16,17},{18,... | collective-permute-start | bytes 18440 | tf_op jit(solution)/shard_map/ppermute | solution.py:17
  19.5 6.0 %collective-permute-start.2 = (f32[3,512]{1,0:T(4,128)S(1)}, f32[3,512]{1,0:T(4,128)S(1)}, u32[]{:S(2)}, u32[]{:S(2)}) collective-permute-start(f32[3,512]{1,0:T(4,128)S(1)} %get-tuple-element.556), channel_id=1, source_target_pairs={{1,0},{3,2},{5,4},{7,6},{9,8},{11,10},{13,12},{15,14},{17,16},{19,... | collective-permute-start | bytes 18440 | tf_op jit(solution)/shard_map/ppermute | solution.py:18
  27.3 5.9 %collective-permute-start.6 = (f32[3,512]{1,0:T(4,128)S(1)}, f32[3,512]{1,0:T(4,128)S(1)}, u32[]{:S(2)}, u32[]{:S(2)}) collective-permute-start(f32[3,512]{1,0:T(4,128)S(1)} %get-tuple-element.554), channel_id=1, source_target_pairs={{1,0},{3,2},{5,4},{7,6},{9,8},{11,10},{13,12},{15,14},{17,16},{19,... | collective-permute-start | bytes 18440 | tf_op jit(solution)/shard_map/ppermute | solution.py:18
  50.7 5.9 %collective-permute-start.12 = (f32[3,512]{1,0:T(4,128)S(1)}, f32[3,512]{1,0:T(4,128)S(1)}, u32[]{:S(2)}, u32[]{:S(2)}) collective-permute-start(f32[3,512]{1,0:T(4,128)S(1)} %get-tuple-element.548), channel_id=1, source_target_pairs={{1,0},{3,2},{5,4},{7,6},{9,8},{11,10},{13,12},{15,14},{17,16},{19,... | collective-permute-start | bytes 18440 | tf_op jit(solution)/shard_map/ppermute | solution.py:18
  74.1 11.7 %collective-permute-start.18 = (f32[3,512]{1,0:T(4,128)S(1)}, f32[3,512]{1,0:T(4,128)S(1)}, u32[]{:S(2)}, u32[]{:S(2)}) collective-permute-start(f32[3,512]{1,0:T(4,128)S(1)} %get-tuple-element.528), channel_id=1, source_target_pairs={{1,0},{3,2},{5,4},{7,6},{9,8},{11,10},{13,12},{15,14},{17,16},{19,... | collective-permute-start | bytes 18440 | tf_op jit(solution)/shard_map/ppermute | solution.py:18
  75.4 10.4 %collective-permute-start.17 = (f32[3,512]{1,0:T(4,128)S(1)}, f32[3,512]{1,0:T(4,128)S(1)}, u32[]{:S(2)}, u32[]{:S(2)}) collective-permute-start(f32[3,512]{1,0:T(4,128)S(1)} %get-tuple-element.527), channel_id=1, source_target_pairs={{0,1},{2,3},{4,5},{6,7},{8,9},{10,11},{12,13},{14,15},{16,17},{18,... | collective-permute-start | bytes 18440 | tf_op jit(solution)/shard_map/ppermute | solution.py:17
  79.9 6.4 %collective-permute-start.27 = (f32[3,512]{1,0:T(4,128)S(1)}, f32[3,512]{1,0:T(4,128)S(1)}, u32[]{:S(2)}, u32[]{:S(2)}) collective-permute-start(f32[3,512]{1,0:T(4,128)S(1)} %get-tuple-element.542), channel_id=1, source_target_pairs={{1,0},{3,2},{5,4},{7,6},{9,8},{11,10},{13,12},{15,14},{17,16},{19,... | collective-permute-start | bytes 18440 | tf_op jit(solution)/shard_map/ppermute | solution.py:18
  118.9 7.2 %collective-permute-start.37 = (f32[3,512]{1,0:T(4,128)S(1)}, f32[3,512]{1,0:T(4,128)S(1)}, u32[]{:S(2)}, u32[]{:S(2)}) collective-permute-start(f32[3,512]{1,0:T(4,128)S(1)} %get-tuple-element.532), channel_id=1, source_target_pairs={{1,0},{3,2},{5,4},{7,6},{9,8},{11,10},{13,12},{15,14},{17,16},{19,... | collective-permute-start | bytes 18440 | tf_op jit(solution)/shard_map/ppermute | solution.py:18
  124.7 7.8 %collective-permute-start.19 = (f32[16,512]{1,0:T(8,128)S(1)}, f32[16,512]{1,0:T(8,128)S(1)}, u32[]{:S(2)}, u32[]{:S(2)}) collective-permute-start(f32[16,512]{1,0:T(8,128)S(1)} %get-tuple-element.288), channel_id=1, source_target_pairs={{0,2},{2,4},{4,6},{6,8},{8,10},{10,12},{12,14},{14,16},{16,18},{18... | collective-permute-start | bytes 98312 | tf_op jit(solution)/shard_map/ppermute | solution.py:26
  126.7 11.1 %collective-permute-start.39 = (f32[3,512]{1,0:T(4,128)S(1)}, f32[3,512]{1,0:T(4,128)S(1)}, u32[]{:S(2)}, u32[]{:S(2)}) collective-permute-start(f32[3,512]{1,0:T(4,128)S(1)} %get-tuple-element.530), channel_id=1, source_target_pairs={{1,0},{3,2},{5,4},{7,6},{9,8},{11,10},{13,12},{15,14},{17,16},{19,... | collective-permute-start | bytes 18440 | tf_op jit(solution)/shard_map/ppermute | solution.py:18
  128.0 9.8 %collective-permute-start.38 = (f32[3,512]{1,0:T(4,128)S(1)}, f32[3,512]{1,0:T(4,128)S(1)}, u32[]{:S(2)}, u32[]{:S(2)}) collective-permute-start(f32[3,512]{1,0:T(4,128)S(1)} %get-tuple-element.529), channel_id=1, source_target_pairs={{0,1},{2,3},{4,5},{6,7},{8,9},{10,11},{12,13},{14,15},{16,17},{18,... | collective-permute-start | bytes 18440 | tf_op jit(solution)/shard_map/ppermute | solution.py:17
  132.5 7.1 %collective-permute-start.20 = (f32[16,512]{1,0:T(8,128)S(1)}, f32[16,512]{1,0:T(8,128)S(1)}, u32[]{:S(2)}, u32[]{:S(2)}) collective-permute-start(f32[16,512]{1,0:T(8,128)S(1)} %multiply_add_fusion.5), channel_id=1, source_target_pairs={{0,4},{2,6},{4,8},{6,10},{8,12},{10,14},{12,16},{14,18},{16,20},{1... | collective-permute-start | bytes 98312 | tf_op jit(solution)/shard_map/ppermute | solution.py:26
  138.3 7.2 %collective-permute-start.40 = (f32[16,512]{1,0:T(8,128)S(1)}, f32[16,512]{1,0:T(8,128)S(1)}, u32[]{:S(2)}, u32[]{:S(2)}) collective-permute-start(f32[16,512]{1,0:T(8,128)S(1)} %fusion.51), channel_id=1, source_target_pairs={{2,0},{4,2},{6,4},{8,6},{10,8},{12,10},{14,12},{16,14},{18,16},{20... | collective-permute-start | bytes 98312 | tf_op jit(solution)/shard_map/ppermute | solution.py:26
  139.7 7.5 %collective-permute-start.21 = (f32[16,512]{1,0:T(8,128)S(1)}, f32[16,512]{1,0:T(8,128)S(1)}, u32[]{:S(2)}, u32[]{:S(2)}) collective-permute-start(f32[16,512]{1,0:T(8,128)S(1)} %multiply_add_fusion.4), channel_id=1, source_target_pairs={{0,8},{2,10},{4,12},{6,14},{8,16},{10,18},{12,20},{14,22},{16,24},... | collective-permute-start | bytes 98312 | tf_op jit(solution)/shard_map/ppermute | solution.py:26
  153.0 6.1 %collective-permute-start.42 = (f32[16,512]{1,0:T(8,128)S(1)}, f32[16,512]{1,0:T(8,128)S(1)}, u32[]{:S(2)}, u32[]{:S(2)}) collective-permute-start(f32[16,512]{1,0:T(8,128)S(1)} %multiply_add_fusion.1), channel_id=1, source_target_pairs={{8,0},{10,2},{12,4},{14,6},{16,8},{18,10},{20,12},{22,14},{24,16},... | collective-permute-start | bytes 98312 | tf_op jit(solution)/shard_map/ppermute | solution.py:26
  159.1 6.8 %collective-permute-start.43 = (f32[16,512]{1,0:T(8,128)S(1)}, f32[16,512]{1,0:T(8,128)S(1)}, u32[]{:S(2)}, u32[]{:S(2)}) collective-permute-start(f32[16,512]{1,0:T(8,128)S(1)} %multiply_add_fusion), channel_id=1, source_target_pairs={{16,0},{18,2},{20,4},{22,6},{24,8},{26,10},{28,12},{30,14},{17,1},... | collective-permute-start | bytes 98312 | tf_op jit(solution)/shard_map/ppermute | solution.py:26
  160.4 7.0 %collective-permute-start.22 = (f32[16,512]{1,0:T(8,128)S(1)}, f32[16,512]{1,0:T(8,128)S(1)}, u32[]{:S(2)}, u32[]{:S(2)}) collective-permute-start(f32[16,512]{1,0:T(8,128)S(1)} %get-tuple-element.525), channel_id=1, source_target_pairs={{0,16},{2,18},{4,20},{6,22},{8,24},{10,26},{12,28},{14,30},{1,17},... | collective-permute-start | bytes 98312 | tf_op jit(solution)/shard_map/ppermute | solution.py:26
  169.1 9.2 %collective-permute-start.46 = (f32[3,512]{1,0:T(4,128)S(1)}, f32[3,512]{1,0:T(4,128)S(1)}, u32[]{:S(2)}, u32[]{:S(2)}) collective-permute-start(f32[3,512]{1,0:T(4,128)S(1)} %get-tuple-element.510), channel_id=1, source_target_pairs={{1,0},{3,2},{5,4},{7,6},{9,8},{11,10},{13,12},{15,14},{17,16},{19,... | collective-permute-start | bytes 18440 | tf_op jit(solution)/shard_map/ppermute | solution.py:18
  170.4 8.0 %collective-permute-start.45 = (f32[3,512]{1,0:T(4,128)S(1)}, f32[3,512]{1,0:T(4,128)S(1)}, u32[]{:S(2)}, u32[]{:S(2)}) collective-permute-start(f32[3,512]{1,0:T(4,128)S(1)} %get-tuple-element.509), channel_id=1, source_target_pairs={{0,1},{2,3},{4,5},{6,7},{8,9},{10,11},{12,13},{14,15},{16,17},{18,... | collective-permute-start | bytes 18440 | tf_op jit(solution)/shard_map/ppermute | solution.py:17
  187.0 5.9 %collective-permute-start.51 = (f32[3,512]{1,0:T(4,128)S(1)}, f32[3,512]{1,0:T(4,128)S(1)}, u32[]{:S(2)}, u32[]{:S(2)}) collective-permute-start(f32[3,512]{1,0:T(4,128)S(1)} %get-tuple-element.522), channel_id=1, source_target_pairs={{1,0},{3,2},{5,4},{7,6},{9,8},{11,10},{13,12},{15,14},{17,16},{19,... | collective-permute-start | bytes 18440 | tf_op jit(solution)/shard_map/ppermute | solution.py:18
  (58 other events, 452.2 us)
where the time goes:
time: 341 us; the launch traced here: 339 us
  starting transfers between devices  213 us (62%)
  blocking collectives  58.3 us (17%)
  waiting for transfers between devices  45.6 us (13%)
  other arithmetic  10.5 us (3%)
  local copies, waits for them, and re-layouts  8.67 us (3%)
    ppermute x31, starting transfers between devices, with_halo(): before = lax.ppermute(last, axis, up)  141 us
    psum x1, blocking collectives, shards(): gradient = lax.psum(adjoint_states + fine_local, 'tm') / steps_total  58.3 us
    ppermute x31, starting transfers between devices, with_halo(): after = lax.ppermute(leading, axis, down)  40.1 us
    ppermute x31, waiting for transfers between devices, with_halo(): before = lax.ppermute(last, axis, up)  32.1 us
    ppermute x12, starting transfers between devices, passed_along(): return lax.ppermute(block, axis, route)  32 us
    ppermute x12, waiting for transfers between devices, passed_along(): return lax.ppermute(block, axis, route)  13.4 us
    slice x90, local copies, waits for them, and re-layouts, neighbours(): source[..., :, 1:]  6.92 us
  transfers between devices with their start and end apart: 74, of which 31 were waited for; matrix products, arithmetic and copies ran while one was open for 1% of the time, Pallas kernels for 0%

commit v1 on v0

v1 whole, which is shorter than its diff:
```python
import functools

import jax
import jax.numpy as jnp
from jax import lax
from jax.experimental import pallas as pl
from jax.experimental.pallas import tpu as pltpu
from jax.sharding import PartitionSpec as P

SWEEPS = 3
COARSEN = 8
SUB, LANES = 8, 128
MESH = pl.DeviceIdType.MESH

CONTROL, DIFFUSION, REACTION, ENTRY, GUESS, TARGET, FORWARD, EXIT, INITIAL, ADJOINT = range(10)
SLOTS = 10
SUM_ENTRY, SUM_STATES, SUM_TARGET, SUM_EXIT, SUM_ADJOINT = range(5)


def kernel(
    T, X,
    control_ref, initial_ref, diffusion_ref, reaction_ref, guess_ref, adjoint_ref, observed_ref,
    states_out, adjoints_out, gradient_out,
    full, weight, inverse, points, total, sums, gathered, gathered_adj, solved, solved_adj,
    packed, packed_adj, landed, landed_adj,
    in_send, in_recv, m1_send, m1_recv, m2_send, m2_recv,
    b1_send, b1_recv, b2_send, b2_recv, p1_send, p1_recv, p2_send, p2_recv,
):
    rows, cols = control_ref.shape
    grid_rows = rows * X
    col_tiles = cols // LANES
    tiles = (grid_rows // SUB) * col_tiles
    own_tiles = (rows // SUB) * col_tiles
    stride = T // tiles
    j = lax.axis_index("tm")
    x = lax.axis_index("space")
    first, last = j == 0, j == T - 1

    def device(tm, space):
        return {"tm": tm, "space": space}

    def side(o):
        return lax.rem(x + o, X)

    def from_side(o):
        return lax.rem(x + X - o, X)

    barrier = pltpu.get_barrier_semaphore()

    def greet(tm, space):
        pl.semaphore_signal(barrier, inc=1, device_id=device(tm, space), device_id_type=MESH)

    def greet_plane(i, c):
        greet(lax.rem(j + i, T), x)
        return c

    for o in range(1, X):
        greet(j, side(o))

        @pl.when(j > 0)
        def _():
            greet(j - 1, side(o))

        @pl.when(j < T - 1)
        def _():
            greet(j + 1, side(o))

    lax.fori_loop(1, T, greet_plane, 0)

    def block_rows(space):
        return pl.ds(pl.multiple_of(space * rows, rows), rows)

    own = block_rows(x)
    full[CONTROL, own, :] = control_ref[...]
    full[DIFFUSION, own, :] = diffusion_ref[...]
    full[REACTION, own, :] = reaction_ref[...]
    full[GUESS, own, :] = guess_ref[0]
    full[TARGET, own, :] = observed_ref[0]
    full[INITIAL, own, :] = initial_ref[...]

    @pl.when(first)
    def _():
        full[ENTRY, own, :] = initial_ref[...]

    @pl.when(last)
    def _():
        full[EXIT] = jnp.zeros((grid_rows, cols), jnp.float32)

    neighbours_count = (j > 0).astype(jnp.int32) + (j < T - 1).astype(jnp.int32)
    pl.semaphore_wait(barrier, (T - 1) + (X - 1) * (1 + neighbours_count))

    def send(src, slot, o, tm):
        return pltpu.make_async_remote_copy(
            src_ref=src, dst_ref=full.at[slot, own, :],
            send_sem=in_send.at[slot, o], recv_sem=in_recv.at[slot, o],
            device_id=device(tm, side(o)), device_id_type=MESH,
        )

    def entry_copy(o):
        return send(guess_ref.at[0], ENTRY, o, j + 1)

    def initial_entry_copy(o):
        return pltpu.make_async_remote_copy(
            src_ref=initial_ref, dst_ref=full.at[ENTRY, own, :],
            send_sem=in_send.at[FORWARD, o], recv_sem=in_recv.at[ENTRY, o],
            device_id=device(j, side(o)), device_id_type=MESH,
        )

    def exit_copy(o):
        return send(adjoint_ref.at[0], EXIT, o, j - 1)

    def input_sends(act):
        for o in range(1, X):
            act(send(diffusion_ref, DIFFUSION, o, j))
            act(send(reaction_ref, REACTION, o, j))
            act(send(control_ref, CONTROL, o, j))

            @pl.when(first)
            def _():
                act(initial_entry_copy(o))

        @pl.when(j < T - 1)
        def _():
            for o in range(X):
                act(entry_copy(o))

        for o in range(1, X):
            act(send(guess_ref.at[0], GUESS, o, j))
            act(send(observed_ref.at[0], TARGET, o, j))

        @pl.when(j > 0)
        def _():
            for o in range(X):
                act(exit_copy(o))

        for o in range(1, X):
            act(send(initial_ref, INITIAL, o, j))

    def await_input(slot, o):
        pltpu.make_async_remote_copy(
            src_ref=control_ref, dst_ref=full.at[slot, block_rows(from_side(o)), :],
            send_sem=in_send.at[slot, o], recv_sem=in_recv.at[slot, o],
            device_id=device(j, side(o)), device_id_type=MESH,
        ).wait_recv()

    input_sends(lambda copy: copy.start())

    lane = lax.broadcasted_iota(jnp.int32, (grid_rows, LANES), 1)
    row = lax.broadcasted_iota(jnp.int32, (grid_rows, LANES), 0)
    lane_low, lane_high = lane == 0, lane == LANES - 1
    row_low, row_high = row == 0, row == grid_rows - 1
    blocks = range(col_tiles)
    zero = jnp.zeros((grid_rows, LANES), jnp.float32)

    def cut(value):
        return [value[:, b * LANES : (b + 1) * LANES] for b in blocks]

    def get(ref, *index):
        return [ref[(*index, slice(None), pl.ds(b * LANES, LANES))] for b in blocks]

    def put(ref, value, *index):
        for b in blocks:
            ref[(*index, slice(None), pl.ds(b * LANES, LANES))] = value[b]

    def zipped(f, *lists):
        return [f(*items) for items in zip(*lists)]

    def neighbours(v):
        right = [pltpu.roll(b, LANES - 1, 1) for b in v]
        left = [pltpu.roll(b, 1, 1) for b in v]
        out = []
        for b in blocks:
            up = jnp.where(row_low, 0.0, pltpu.roll(v[b], 1, 0))
            down = jnp.where(row_high, 0.0, pltpu.roll(v[b], grid_rows - 1, 0))
            to_right = jnp.where(lane_high, right[b + 1] if b + 1 < col_tiles else zero, right[b])
            to_left = jnp.where(lane_low, left[b - 1] if b > 0 else zero, left[b])
            out.append((up + down) + (to_right + to_left))
        return out

    def forward_step(v, scale):
        rhs = zipped(lambda a, c: a + scale * c, v, get(full, CONTROL))
        w = get(weight)
        base = zipped(lambda a, c: a * c, rhs, get(inverse))
        iterate = rhs
        for _ in range(SWEEPS):
            iterate = zipped(lambda a, c, n: a + c * n, base, w, neighbours(iterate))
        return iterate

    def adjoint_step(y):
        w = get(weight)
        carried, summed = y, y
        for _ in range(SWEEPS - 1):
            carried = neighbours(zipped(lambda a, c: a * c, w, carried))
            summed = zipped(lambda a, c: a + c, summed, carried)
        tail = neighbours(zipped(lambda a, c: a * c, w, carried))
        return zipped(lambda a, c, t: a * c + t, summed, get(inverse), tail)

    def misfit_added(g, point, target):
        return zipped(lambda a, p, o: a + (p - o) * (1.0 / COARSEN), g, point, target)

    for o in range(1, X):
        await_input(DIFFUSION, o)
        await_input(REACTION, o)
    spread = full[DIFFUSION]
    diagonal = 1.0 + 4.0 * spread + full[REACTION]
    reciprocal = 1.0 / diagonal
    inverse[...] = reciprocal
    weight[...] = spread * reciprocal

    def forward_points(start, scale):
        def body(i, v):
            v = forward_step(v, scale)
            put(points, v, i)
            return v

        return lax.fori_loop(0, COARSEN - 1, body, start)

    for o in range(1, X):
        await_input(CONTROL, o)
        await_input(ENTRY, o)

    @pl.when(j > 0)
    def _():
        await_input(ENTRY, 0)

    damping = 1.0 / (1.0 + COARSEN * full[REACTION])

    v = forward_points(get(full, ENTRY), 1.0)
    v = forward_step(v, 1.0)
    keep = (j > 0).astype(jnp.float32)
    put(full, zipped(lambda a, d, s: a - keep * (d * s), v, cut(damping), get(full, ENTRY)), FORWARD)

    for o in range(1, X):
        await_input(GUESS, o)
        await_input(TARGET, o)
        await_input(INITIAL, o)

    def tile_rows(d):
        return pl.ds(pl.multiple_of((d // col_tiles) * SUB, SUB), SUB)

    def tile_cols(d):
        return pl.ds(pl.multiple_of(lax.rem(d, col_tiles) * LANES, LANES), LANES)

    mine = j // stride
    owner = jnp.logical_and(lax.rem(j, stride) == 0, mine < tiles)
    my_rows, my_cols = tile_rows(lax.rem(mine, tiles)), tile_cols(lax.rem(mine, tiles))

    def scatter(act, source, target, send_sem, recv_sem):
        def body(i, c):
            d = lax.rem(mine + i, tiles)

            @pl.when(d * stride != j)
            def _():
                act(pltpu.make_async_remote_copy(
                    src_ref=source(tile_rows(d), tile_cols(d)), dst_ref=target.at[j],
                    send_sem=send_sem.at[d], recv_sem=recv_sem.at[j],
                    device_id=device(d * stride, x), device_id_type=MESH,
                ))

            return c

        lax.fori_loop(0, tiles, body, 0)

    def source_forward(r, c):
        return full.at[pl.ds(TARGET, 2), r, c]

    def source_adjoint(r, c):
        return full.at[ADJOINT, r, c]

    def await_gather(source, target, send_sem, recv_sem):
        def body(i, c):
            k = lax.rem(j + i, T)
            pltpu.make_async_remote_copy(
                src_ref=source(my_rows, my_cols), dst_ref=target.at[k],
                send_sem=send_sem.at[0], recv_sem=recv_sem.at[k],
                device_id=device(k, x), device_id_type=MESH,
            ).wait_recv()
            return c

        lax.fori_loop(1, T, body, 0)

    def spread_sums(act, source, slot, count, send_sem, recv_sem):
        def body(i, c):
            k = lax.rem(j + i, T)
            act(pltpu.make_async_remote_copy(
                src_ref=source, dst_ref=sums.at[pl.ds(slot, count), my_rows, my_cols],
                send_sem=send_sem.at[k], recv_sem=recv_sem.at[mine],
                device_id=device(k, x), device_id_type=MESH,
            ))
            return c

        lax.fori_loop(1, T, body, 0)

    def await_sums(source, slot, count, send_sem, recv_sem):
        def body(d, c):
            @pl.when(d * stride != j)
            def _():
                pltpu.make_async_remote_copy(
                    src_ref=source, dst_ref=sums.at[pl.ds(slot, count), tile_rows(d), tile_cols(d)],
                    send_sem=send_sem.at[0], recv_sem=recv_sem.at[d],
                    device_id=device(d * stride, x), device_id_type=MESH,
                ).wait_recv()

            return c

        lax.fori_loop(0, tiles, body, 0)

    local = mine - x * own_tiles
    holds_output = jnp.logical_and(owner, jnp.logical_and(local >= 0, local < own_tiles))
    local_tile = lax.rem(local + tiles, own_tiles)

    def spread_solved(act, source, target, send_sem, recv_sem):
        def body(i, c):
            k = lax.rem(j + i, T)
            act(pltpu.make_async_remote_copy(
                src_ref=source.at[k], dst_ref=target.at[tile_rows(local_tile), tile_cols(local_tile)],
                send_sem=send_sem.at[k], recv_sem=recv_sem.at[local_tile],
                device_id=device(k, x), device_id_type=MESH,
            ))
            return c

        lax.fori_loop(1, T, body, 0)

    def await_solved(source, target, send_sem, recv_sem):
        def body(d, c):
            source_tm = (d + x * own_tiles) * stride

            @pl.when(source_tm != j)
            def _():
                pltpu.make_async_remote_copy(
                    src_ref=source.at[0], dst_ref=target.at[tile_rows(d), tile_cols(d)],
                    send_sem=send_sem.at[0], recv_sem=recv_sem.at[d],
                    device_id=device(source_tm, x), device_id_type=MESH,
                ).wait_recv()

            return c

        lax.fori_loop(0, own_tiles, body, 0)

    start = lambda copy: copy.start()
    finish = lambda copy: copy.wait_send()

    scatter(start, source_forward, gathered, m1_send, m1_recv)

    @pl.when(j < T - 1)
    def _():
        for o in range(X):
            await_input(EXIT, o)

    def adjoint_points(g, target):
        def body(i, g):
            at = COARSEN - 2 - i
            return adjoint_step(misfit_added(g, get(points, at), get(*target)))

        return body

    g = adjoint_step(misfit_added(get(full, EXIT), get(full, GUESS), get(full, TARGET)))
    g = lax.fori_loop(0, COARSEN - 1, adjoint_points(g, (full, TARGET)), g)
    put(full, zipped(lambda a, d, t: a - d * t, g, cut(damping), get(full, EXIT)), ADJOINT)
    scatter(start, source_adjoint, gathered_adj, m2_send, m2_recv)

    @pl.when(owner)
    def _():
        my_damping = 1.0 / (1.0 + COARSEN * full[REACTION, my_rows, my_cols])
        gathered[j] = full[pl.ds(TARGET, 2), my_rows, my_cols]
        await_gather(source_forward, gathered, m1_send, m1_recv)

        def body(k, carry):
            state, before, through, target = carry
            state = my_damping * state + gathered[k, 1]
            solved[k] = state
            return (state, through, through + state, target + gathered[k, 0])

        head = gathered[0, 1]
        solved[0] = head
        _, before, through, target = lax.fori_loop(1, T, body, (head, head, head, gathered[0, 0]))
        for slot, value in ((SUM_ENTRY, before), (SUM_STATES, through), (SUM_TARGET, target)):
            packed[slot] = value
            sums[slot, my_rows, my_cols] = value
        spread_sums(start, packed, SUM_ENTRY, 3, b1_send, b1_recv)

    @pl.when(holds_output)
    def _():
        spread_solved(start, solved, landed, p1_send, p1_recv)
        landed[tile_rows(local_tile), tile_cols(local_tile)] = solved[j]

    @pl.when(owner)
    def _():
        my_damping = 1.0 / (1.0 + COARSEN * full[REACTION, my_rows, my_cols])
        gathered_adj[j] = full[ADJOINT, my_rows, my_cols]
        await_gather(source_adjoint, gathered_adj, m2_send, m2_recv)

        def body(i, carry):
            k = T - 1 - i
            state, before, through = carry
            state = my_damping * state + gathered_adj[k]
            solved_adj[k] = state
            return (state, through, through + state)

        head = gathered_adj[T - 1]
        solved_adj[T - 1] = head
        _, before, through = lax.fori_loop(1, T, body, (head,) * 3)
        for slot, value in ((SUM_EXIT, before), (SUM_ADJOINT, through)):
            packed_adj[slot - SUM_EXIT] = value
            sums[slot, my_rows, my_cols] = value
        spread_sums(start, packed_adj, SUM_EXIT, 2, b2_send, b2_recv)

    @pl.when(holds_output)
    def _():
        spread_solved(start, solved_adj, landed_adj, p2_send, p2_recv)
        landed_adj[tile_rows(local_tile), tile_cols(local_tile)] = solved_adj[j]

    await_sums(packed, SUM_ENTRY, 3, b1_send, b1_recv)
    entry_sum = zipped(lambda a, c: a + c, get(sums, SUM_ENTRY), get(full, INITIAL))
    forward_points(entry_sum, float(T))
    await_solved(solved, landed, p1_send, p1_recv)
    states_out[0] = landed[...]

    await_sums(packed_adj, SUM_EXIT, 2, b2_send, b2_recv)
    g = adjoint_step(misfit_added(get(sums, SUM_EXIT), get(sums, SUM_STATES), get(sums, SUM_TARGET)))
    put(total, zipped(lambda a, c: a + c, get(sums, SUM_ADJOINT), g))

    def final_body(i, g):
        g = adjoint_points(g, (sums, SUM_TARGET))(i, g)
        put(total, zipped(lambda a, c: a + c, get(total), g))
        return g

    lax.fori_loop(0, COARSEN - 2, final_body, g)
    gradient_out[...] = total[own, :] * (1.0 / (COARSEN * T))
    await_solved(solved_adj, landed_adj, p2_send, p2_recv)
    adjoints_out[0] = landed_adj[...]

    input_sends(finish)
    scatter(finish, source_forward, gathered, m1_send, m1_recv)
    scatter(finish, source_adjoint, gathered_adj, m2_send, m2_recv)

    @pl.when(owner)
    def _():
        spread_sums(finish, packed, SUM_ENTRY, 3, b1_send, b1_recv)
        spread_sums(finish, packed_adj, SUM_EXIT, 2, b2_send, b2_recv)

    @pl.when(holds_output)
    def _():
        spread_solved(finish, solved, landed, p1_send, p1_recv)
        spread_solved(finish, solved_adj, landed_adj, p2_send, p2_recv)


def solution(mesh):
    T, X = mesh.shape["tm"], mesh.shape["space"]

    def shards(control, initial, diffusion, reaction, forward_guess, adjoint_guess, observed):
        rows, cols = control.shape
        grid_rows = rows * X
        tiles = (grid_rows // SUB) * (cols // LANES)
        own_tiles = (rows // SUB) * (cols // LANES)
        vmem = pl.BlockSpec(memory_space=pltpu.VMEM)
        f32 = lambda *shape: pltpu.VMEM(shape, jnp.float32)
        dma = lambda *shape: pltpu.SemaphoreType.DMA(shape)
        return pl.pallas_call(
            functools.partial(kernel, T, X),
            out_shape=(
                jax.ShapeDtypeStruct(forward_guess.shape, jnp.float32),
                jax.ShapeDtypeStruct(forward_guess.shape, jnp.float32),
                jax.ShapeDtypeStruct(control.shape, jnp.float32),
            ),
            in_specs=[vmem] * 7,
            out_specs=(vmem,) * 3,
            scratch_shapes=[
                f32(SLOTS, grid_rows, cols),
                f32(grid_rows, cols),
                f32(grid_rows, cols),
                f32(COARSEN - 1, grid_rows, cols),
                f32(grid_rows, cols),
                f32(5, grid_rows, cols),
                f32(T, 2, SUB, LANES),
                f32(T, SUB, LANES),
                f32(T, SUB, LANES),
                f32(T, SUB, LANES),
                f32(3, SUB, LANES),
                f32(2, SUB, LANES),
                f32(rows, cols),
                f32(rows, cols),
                dma(SLOTS, X), dma(SLOTS, X),
                dma(tiles), dma(T), dma(tiles), dma(T),
                dma(T), dma(tiles), dma(T), dma(tiles),
                dma(T), dma(own_tiles), dma(T), dma(own_tiles),
            ],
            compiler_params=pltpu.CompilerParams(collective_id=0, has_side_effects=True),
        )(control, initial, diffusion, reaction, forward_guess, adjoint_guess, observed)

    return jax.shard_map(
        shards,
        mesh=mesh,
        in_specs=(
            P("space", None),
            P("space", None),
            P("space", None),
            P("space", None),
            P("tm", "space", None),
            P("tm", "space", None),
            P("tm", "space", None),
        ),
        out_specs=(P("tm", "space", None), P("tm", "space", None), P("space", None)),
        check_vma=False,
    )
```

time: 341 us -> 38.6 us (0.11)
  starting transfers between devices: 213 us -> 0 us
  blocking collectives: 58.3 us -> 0 us
  waiting for transfers between devices: 45.6 us -> 0 us
  Pallas kernels: 0 us -> 34.5 us
  other arithmetic: 10.5 us -> 0 us
  local copies, waits for them, and re-layouts: 8.67 us -> 2.77 us
    ppermute x74 -> x0, starting transfers between devices: 213 us -> none  [the longest x31 141 us: with_halo(): before = lax.ppermute(last, axis, up)]
    psum x1 -> x0, blocking collectives: 58.3 us -> none  [shards(): gradient = lax.psum(adjoint_states + fine_local, 'tm') / steps_total]
    ppermute x74 -> x0, waiting for transfers between devices: 45.6 us -> none  [the longest x31 32.1 us: with_halo(): before = lax.ppermute(last, axis, up)]
    pallas_call x0 -> x1, Pallas kernels: none -> 34.5 us  [shards(): pl.pallas_call(functools.partial(kernel, T, X), out_shape=(jax.ShapeDtype...]
    slice x210 -> x0, local copies, waits for them, and re-layouts: 7.9 us -> none  [the longest x90 6.92 us: neighbours(): source[..., :, 1:]]
  transfers between devices with their start and end apart: 74 -> 0, of which waited for: 31 -> 0; matrix products, arithmetic and copies ran while one was open for 1% -> 0% of each run, Pallas kernels for 0% -> 0%
where the time goes in v1:
time: 38.6 us; the launch traced here: 37.9 us
  Pallas kernels  34.5 us (89%)
  local copies, waits for them, and re-layouts  2.77 us (7%)
  between operations  0.65 us (2%)
    pallas_call x1, Pallas kernels, shards(): pl.pallas_call(functools.partial(kernel, T, X), out_shape=(jax.ShapeDtype...  34.5 us
    unnamed x7, local copies, waits for them, and re-layouts  2.77 us

profile of v1, /device:TPU:0, one launch (start us, length us, event | category | flops | bytes accessed | tf_op | source)
XLA Modules:
  0.0 37.9 jit_solution(14334496097916759926)
XLA Ops:
  0.6 34.5 %shard_map.94 = (f32[1,16,512]{2,1,0:T(8,128)}, f32[1,16,512]{2,1,0:T(8,128)}, f32[16,512]{1,0:T(8,128)}) custom-call(f32[16,512]{1,0:T(8,128)} %control_ref.1, f32[16,512]{1,0:T(8,128)} %initial_ref.1, f32[16,512]{1,0:T(8,128)} %diffusion_ref.1, f32[16,512]{1,0:T(8,128)} %reaction_ref.1, f32[1,16,512]{2,1,0:T(8,128)} %guess_ref.1, ...), custom_call_target="tpu_custom_call" | custom-call | tf_op jit(solution)/shard_map/pallas_call | solution.py:459
  35.2 0.0 copy-start.1
  35.2 1.4 %copy.13 = f32[1,16,512]{2,1,0:T(8,128)} copy(f32[1,16,512]{2,1,0:T(8,128)} %get-tuple-element.6) | data formatting | bytes 65536
  36.5 0.0 copy-done.1
  36.6 0.0 copy-start
  36.6 0.6 %copy.14 = f32[1,16,512]{2,1,0:T(8,128)} copy(f32[1,16,512]{2,1,0:T(8,128)S(1)} %copy-done.1) | data formatting | bytes 65536
  37.2 0.2 copy-done
  37.3 0.6 %copy.15 = f32[16,512]{1,0:T(8,128)} copy(f32[16,512]{1,0:T(8,128)S(1)} %copy-done) | data formatting | bytes 65536
Async XLA Ops:
  35.2 1.4 %copy-start.1 = (f32[1,16,512]{2,1,0:T(8,128)S(1)}, f32[1,16,512]{2,1,0:T(8,128)}, u32[]{:S(2)}) copy-start(f32[1,16,512]{2,1,0:T(8,128)} %get-tuple-element.7) | copy-start | bytes 98308
  36.6 0.8 %copy-start = (f32[16,512]{1,0:T(8,128)S(1)}, f32[16,512]{1,0:T(8,128)}, u32[]{:S(2)}) copy-start(f32[16,512]{1,0:T(8,128)} %get-tuple-element.8) | copy-start | bytes 98308

commit v2 on v1

v2 whole, which is shorter than its diff:
```python
import functools

import jax
import jax.numpy as jnp
from jax import lax
from jax.experimental import pallas as pl
from jax.experimental.pallas import tpu as pltpu
from jax.sharding import PartitionSpec as P

SWEEPS = 3
COARSEN = 8
SUB, LANES = 8, 128
MESH = pl.DeviceIdType.MESH

CONTROL, DIFFUSION, REACTION, ENTRY, GUESS, TARGET, FORWARD, EXIT, INITIAL, ADJOINT = range(10)
SLOTS = 10
SUM_TARGET, SUM_ENTRY, SUM_EXIT = range(3)
SUMS = 3


def kernel(
    T, X,
    control_ref, initial_ref, diffusion_ref, reaction_ref, guess_ref, adjoint_ref, observed_ref,
    states_out, adjoints_out, gradient_out,
    full, own_adjoint, weight, inverse, points, total, sums,
    gathered_target, gathered, gathered_adj, solved, solved_adj, packed, landed, landed_adj,
    local_sem, reach, in_send, in_recv, m0_send, m0_recv, m1_send, m1_recv, m2_send, m2_recv,
    b0_send, b0_recv, b1_send, b1_recv, b2_send, b2_recv, p1_send, p1_recv, p2_send, p2_recv,
):
    rows, cols = control_ref.shape
    grid_rows = rows * X
    col_tiles = cols // LANES
    tiles = (grid_rows // SUB) * col_tiles
    own_tiles = (rows // SUB) * col_tiles
    stride = T // tiles
    j = lax.axis_index("tm")
    x = lax.axis_index("space")
    first, last = j == 0, j == T - 1

    def device(tm, space):
        return {"tm": tm, "space": space}

    def side(o):
        return lax.rem(x + o, X)

    def from_side(o):
        return lax.rem(x + X - o, X)

    def block_rows(space):
        return pl.ds(pl.multiple_of(space * rows, rows), rows)

    own = block_rows(x)

    barrier = pltpu.get_barrier_semaphore()

    def greet(tm, space):
        pl.semaphore_signal(barrier, inc=1, device_id=device(tm, space), device_id_type=MESH)

    for o in range(1, X):
        greet(j, side(o))
    for o in range(X):
        @pl.when(j > 0)
        def _():
            greet(j - 1, side(o))

        @pl.when(j < T - 1)
        def _():
            greet(j + 1, side(o))

    loads = [
        pltpu.make_async_copy(src, dst, local_sem.at[n])
        for n, (src, dst) in enumerate((
            (diffusion_ref, full.at[DIFFUSION, own, :]),
            (reaction_ref, full.at[REACTION, own, :]),
            (control_ref, full.at[CONTROL, own, :]),
            (guess_ref.at[0], full.at[GUESS, own, :]),
            (observed_ref.at[0], full.at[TARGET, own, :]),
            (adjoint_ref.at[0], own_adjoint),
            (initial_ref, full.at[INITIAL, own, :]),
        ))
    ]
    entry_load = pltpu.make_async_copy(initial_ref, full.at[ENTRY, own, :], local_sem.at[len(loads)])

    for copy in loads:
        copy.start()

    @pl.when(first)
    def _():
        entry_load.start()

    @pl.when(last)
    def _():
        full[EXIT] = jnp.zeros((grid_rows, cols), jnp.float32)

    for copy in loads:
        copy.wait()

    @pl.when(first)
    def _():
        entry_load.wait()

    neighbours_count = (j > 0).astype(jnp.int32) + (j < T - 1).astype(jnp.int32)
    pl.semaphore_wait(barrier, (X - 1) + X * neighbours_count)

    rounds = (T - 2).bit_length()

    def reach_out(r):
        h = 1 << r

        @pl.when(j >= h)
        def _():
            pl.semaphore_signal(reach.at[r], inc=1, device_id=device(j - h, x), device_id_type=MESH)

        @pl.when(j < T - h)
        def _():
            pl.semaphore_signal(reach.at[r], inc=1, device_id=device(j + h, x), device_id_type=MESH)

    def reached(r):
        h = 1 << r
        pl.semaphore_wait(reach.at[r], (j >= h).astype(jnp.int32) + (j < T - h).astype(jnp.int32))

    def send(src, slot, o, tm):
        return pltpu.make_async_remote_copy(
            src_ref=src, dst_ref=full.at[slot, own, :],
            send_sem=in_send.at[slot, o], recv_sem=in_recv.at[slot, o],
            device_id=device(tm, side(o)), device_id_type=MESH,
        )

    def mine_of(slot):
        return full.at[slot, own, :]

    def initial_entry_copy(o):
        return pltpu.make_async_remote_copy(
            src_ref=mine_of(INITIAL), dst_ref=full.at[ENTRY, own, :],
            send_sem=in_send.at[FORWARD, o], recv_sem=in_recv.at[ENTRY, o],
            device_id=device(j, side(o)), device_id_type=MESH,
        )

    def input_sends(act):
        for o in range(1, X):
            for slot in (DIFFUSION, REACTION, CONTROL):
                act(send(mine_of(slot), slot, o, j))

            @pl.when(first)
            def _():
                act(initial_entry_copy(o))

        @pl.when(j < T - 1)
        def _():
            for o in range(X):
                act(send(mine_of(GUESS), ENTRY, o, j + 1))

        for o in range(1, X):
            for slot in (TARGET, GUESS):
                act(send(mine_of(slot), slot, o, j))

        @pl.when(j > 0)
        def _():
            for o in range(X):
                act(send(own_adjoint, EXIT, o, j - 1))

        for o in range(1, X):
            act(send(mine_of(INITIAL), INITIAL, o, j))

    def await_input(slot, o):
        pltpu.make_async_remote_copy(
            src_ref=own_adjoint, dst_ref=full.at[slot, block_rows(from_side(o)), :],
            send_sem=in_send.at[slot, o], recv_sem=in_recv.at[slot, o],
            device_id=device(j, side(o)), device_id_type=MESH,
        ).wait_recv()

    input_sends(lambda copy: copy.start())
    reach_out(0)

    lane = lax.broadcasted_iota(jnp.int32, (grid_rows, LANES), 1)
    row = lax.broadcasted_iota(jnp.int32, (grid_rows, LANES), 0)
    lane_low, lane_high = lane == 0, lane == LANES - 1
    row_low, row_high = row == 0, row == grid_rows - 1
    blocks = range(col_tiles)
    zero = jnp.zeros((grid_rows, LANES), jnp.float32)

    def cut(value):
        return [value[:, b * LANES : (b + 1) * LANES] for b in blocks]

    def get(ref, *index):
        return [ref[(*index, slice(None), pl.ds(b * LANES, LANES))] for b in blocks]

    def put(ref, value, *index):
        for b in blocks:
            ref[(*index, slice(None), pl.ds(b * LANES, LANES))] = value[b]

    def zipped(f, *lists):
        return [f(*items) for items in zip(*lists)]

    def neighbours(v):
        right = [pltpu.roll(b, LANES - 1, 1) for b in v]
        left = [pltpu.roll(b, 1, 1) for b in v]
        out = []
        for b in blocks:
            up = jnp.where(row_low, 0.0, pltpu.roll(v[b], 1, 0))
            down = jnp.where(row_high, 0.0, pltpu.roll(v[b], grid_rows - 1, 0))
            to_right = jnp.where(lane_high, right[b + 1] if b + 1 < col_tiles else zero, right[b])
            to_left = jnp.where(lane_low, left[b - 1] if b > 0 else zero, left[b])
            out.append((up + down) + (to_right + to_left))
        return out

    def forward_step(v, scale):
        rhs = zipped(lambda a, c: a + scale * c, v, get(full, CONTROL))
        w = get(weight)
        base = zipped(lambda a, c: a * c, rhs, get(inverse))
        iterate = rhs
        for _ in range(SWEEPS):
            iterate = zipped(lambda a, c, n: a + c * n, base, w, neighbours(iterate))
        return iterate

    def adjoint_step(y):
        w = get(weight)
        carried, summed = y, y
        for _ in range(SWEEPS - 1):
            carried = neighbours(zipped(lambda a, c: a * c, w, carried))
            summed = zipped(lambda a, c: a + c, summed, carried)
        tail = neighbours(zipped(lambda a, c: a * c, w, carried))
        return zipped(lambda a, c, t: a * c + t, summed, get(inverse), tail)

    def misfit_added(g, point, target):
        return zipped(lambda a, p, o: a + (p - o) * (1.0 / COARSEN), g, point, target)

    for o in range(1, X):
        await_input(DIFFUSION, o)
        await_input(REACTION, o)
    reached(0)
    if rounds > 1:
        reach_out(1)
    spread = full[DIFFUSION]
    diagonal = 1.0 + 4.0 * spread + full[REACTION]
    reciprocal = 1.0 / diagonal
    inverse[...] = reciprocal
    weight[...] = spread * reciprocal

    def tile_rows(d):
        return pl.ds(pl.multiple_of((d // col_tiles) * SUB, SUB), SUB)

    def tile_cols(d):
        return pl.ds(pl.multiple_of(lax.rem(d, col_tiles) * LANES, LANES), LANES)

    mine = j // stride
    owner = jnp.logical_and(lax.rem(j, stride) == 0, mine < tiles)
    my_rows, my_cols = tile_rows(lax.rem(mine, tiles)), tile_cols(lax.rem(mine, tiles))

    def scatter(act, slot, target, send_sem, recv_sem):
        def body(i, c):
            d = lax.rem(mine + i, tiles)

            @pl.when(d * stride != j)
            def _():
                act(pltpu.make_async_remote_copy(
                    src_ref=full.at[slot, tile_rows(d), tile_cols(d)], dst_ref=target.at[j],
                    send_sem=send_sem.at[d], recv_sem=recv_sem.at[j],
                    device_id=device(d * stride, x), device_id_type=MESH,
                ))

            return c

        lax.fori_loop(0, tiles, body, 0)

    def await_gather(slot, target, send_sem, recv_sem):
        target[j] = full[slot, my_rows, my_cols]

        def body(i, c):
            k = lax.rem(j + i, T)
            pltpu.make_async_remote_copy(
                src_ref=full.at[slot, my_rows, my_cols], dst_ref=target.at[k],
                send_sem=send_sem.at[0], recv_sem=recv_sem.at[k],
                device_id=device(k, x), device_id_type=MESH,
            ).wait_recv()
            return c

        lax.fori_loop(1, T, body, 0)

    def spread_sums(act, slot, send_sem, recv_sem):
        def body(i, c):
            k = lax.rem(j + i, T)
            act(pltpu.make_async_remote_copy(
                src_ref=packed.at[slot], dst_ref=sums.at[slot, my_rows, my_cols],
                send_sem=send_sem.at[k], recv_sem=recv_sem.at[mine],
                device_id=device(k, x), device_id_type=MESH,
            ))
            return c

        lax.fori_loop(1, T, body, 0)

    def await_sums(slot, send_sem, recv_sem):
        def body(d, c):
            @pl.when(d * stride != j)
            def _():
                pltpu.make_async_remote_copy(
                    src_ref=packed.at[slot], dst_ref=sums.at[slot, tile_rows(d), tile_cols(d)],
                    send_sem=send_sem.at[0], recv_sem=recv_sem.at[d],
                    device_id=device(d * stride, x), device_id_type=MESH,
                ).wait_recv()

            return c

        lax.fori_loop(0, tiles, body, 0)

    local = mine - x * own_tiles
    holds_output = jnp.logical_and(owner, jnp.logical_and(local >= 0, local < own_tiles))
    local_tile = lax.rem(local + tiles, own_tiles)

    def spread_solved(act, source, landing, send_sem, recv_sem):
        def body(i, c):
            k = lax.rem(j + i, T)
            act(pltpu.make_async_remote_copy(
                src_ref=source.at[k], dst_ref=landing(local_tile),
                send_sem=send_sem.at[k], recv_sem=recv_sem.at[local_tile],
                device_id=device(k, x), device_id_type=MESH,
            ))
            return c

        lax.fori_loop(1, T, body, 0)

    def await_solved(source, landing, send_sem, recv_sem):
        def body(d, c):
            source_tm = (d + x * own_tiles) * stride

            @pl.when(source_tm != j)
            def _():
                pltpu.make_async_remote_copy(
                    src_ref=source.at[0], dst_ref=landing(d),
                    send_sem=send_sem.at[0], recv_sem=recv_sem.at[d],
                    device_id=device(source_tm, x), device_id_type=MESH,
                ).wait_recv()

            return c

        lax.fori_loop(0, own_tiles, body, 0)

    def landing(d):
        return landed.at[tile_rows(d), tile_cols(d)]

    def landing_adj(d):
        return landed_adj.at[:, tile_rows(d), tile_cols(d)]

    start = lambda copy: copy.start()
    finish = lambda copy: copy.wait_send()

    def forward_points(start, scale, beside=None):
        def body(i, v):
            v = forward_step(v, scale)
            put(points, v, i)
            if beside is not None:
                beside(i)
            return v

        return lax.fori_loop(0, COARSEN - 1, body, start)

    for o in range(1, X):
        await_input(CONTROL, o)
        await_input(ENTRY, o)

    @pl.when(j > 0)
    def _():
        await_input(ENTRY, 0)

    if rounds > 1:
        reached(1)
    if rounds > 2:
        reach_out(2)
    damping = 1.0 / (1.0 + COARSEN * full[REACTION])
    share_at = 3

    def beside_forward(i):
        for r in range(3, rounds):
            @pl.when(i == ((r - 3) * share_at) // (rounds - 3))
            def _():
                reached(r - 1)
                reach_out(r)

        @pl.when(i == share_at)
        def _():
            if rounds > 2:
                reached(rounds - 1)
            for o in range(1, X):
                await_input(TARGET, o)
            scatter(start, TARGET, gathered_target, m0_send, m0_recv)

    v = forward_points(get(full, ENTRY), 1.0, beside_forward)
    v = forward_step(v, 1.0)
    keep = (j > 0).astype(jnp.float32)
    put(full, zipped(lambda a, d, s: a - keep * (d * s), v, cut(damping), get(full, ENTRY)), FORWARD)
    scatter(start, FORWARD, gathered, m1_send, m1_recv)

    for o in range(1, X):
        await_input(GUESS, o)
        await_input(INITIAL, o)

    @pl.when(j < T - 1)
    def _():
        for o in range(X):
            await_input(EXIT, o)

    def adjoint_points(g, target):
        def body(i, g):
            at = COARSEN - 2 - i
            return adjoint_step(misfit_added(g, get(points, at), get(*target)))

        return body

    g = adjoint_step(misfit_added(get(full, EXIT), get(full, GUESS), get(full, TARGET)))
    g = lax.fori_loop(0, COARSEN - 1, adjoint_points(g, (full, TARGET)), g)
    put(full, zipped(lambda a, d, t: a - d * t, g, cut(damping), get(full, EXIT)), ADJOINT)
    scatter(start, ADJOINT, gathered_adj, m2_send, m2_recv)

    @pl.when(owner)
    def _():
        def share(slot, value, send_sem, recv_sem):
            packed[slot] = value
            sums[slot, my_rows, my_cols] = value
            spread_sums(start, slot, send_sem, recv_sem)

        my_damping = 1.0 / (1.0 + COARSEN * full[REACTION, my_rows, my_cols])

        await_gather(TARGET, gathered_target, m0_send, m0_recv)
        target = lax.fori_loop(1, T, lambda k, c: c + gathered_target[k], gathered_target[0])
        share(SUM_TARGET, target, b0_send, b0_recv)

        await_gather(FORWARD, gathered, m1_send, m1_recv)

        def forward_body(k, carry):
            state, before, through = carry
            state = my_damping * state + gathered[k]
            solved[k] = state
            return (state, through, through + state)

        head = gathered[0]
        solved[0] = head
        _, before, states = lax.fori_loop(1, T, forward_body, (head,) * 3)
        share(SUM_ENTRY, before, b1_send, b1_recv)

        await_gather(ADJOINT, gathered_adj, m2_send, m2_recv)

        def adjoint_body(i, carry):
            k = T - 1 - i
            state, before, through = carry
            state = my_damping * state + gathered_adj[k]
            solved_adj[k, 0] = state
            return (state, through, through + state)

        head = gathered_adj[T - 1]
        solved_adj[T - 1, 0] = head
        _, before, adjoints = lax.fori_loop(1, T, adjoint_body, (head,) * 3)
        share(SUM_EXIT, before + (states - target) * (1.0 / COARSEN), b2_send, b2_recv)

        def fill(k, c):
            solved_adj[k, 1] = adjoints
            return c

        lax.fori_loop(0, T, fill, 0)

    @pl.when(holds_output)
    def _():
        spread_solved(start, solved_adj, landing_adj, p2_send, p2_recv)
        spread_solved(start, solved, landing, p1_send, p1_recv)
        landed_adj[:, tile_rows(local_tile), tile_cols(local_tile)] = solved_adj[j]
        landed[tile_rows(local_tile), tile_cols(local_tile)] = solved[j]

    await_sums(SUM_ENTRY, b1_send, b1_recv)
    entry_sum = zipped(lambda a, c: a + c, get(sums, SUM_ENTRY), get(full, INITIAL))
    forward_points(entry_sum, float(T))

    await_sums(SUM_TARGET, b0_send, b0_recv)
    await_sums(SUM_EXIT, b2_send, b2_recv)
    g = adjoint_step(get(sums, SUM_EXIT))
    put(total, g)

    def final_body(i, g):
        g = adjoint_points(g, (sums, SUM_TARGET))(i, g)
        put(total, zipped(lambda a, c: a + c, get(total), g))
        return g

    lax.fori_loop(0, COARSEN - 2, final_body, g)
    await_solved(solved_adj, landing_adj, p2_send, p2_recv)
    gradient_out[...] = (landed_adj[1] + total[own, :]) * (1.0 / (COARSEN * T))
    adjoints_out[0] = landed_adj[0]
    await_solved(solved, landing, p1_send, p1_recv)
    states_out[0] = landed[...]

    input_sends(finish)
    scatter(finish, TARGET, gathered_target, m0_send, m0_recv)
    scatter(finish, FORWARD, gathered, m1_send, m1_recv)
    scatter(finish, ADJOINT, gathered_adj, m2_send, m2_recv)

    @pl.when(owner)
    def _():
        spread_sums(finish, SUM_TARGET, b0_send, b0_recv)
        spread_sums(finish, SUM_ENTRY, b1_send, b1_recv)
        spread_sums(finish, SUM_EXIT, b2_send, b2_recv)

    @pl.when(holds_output)
    def _():
        spread_solved(finish, solved_adj, landing_adj, p2_send, p2_recv)
        spread_solved(finish, solved, landing, p1_send, p1_recv)


def emit(*refs):
    for source, target in zip(refs[:3], refs[3:]):
        target[...] = source[...]


def solution(mesh):
    T, X = mesh.shape["tm"], mesh.shape["space"]

    def shards(control, initial, diffusion, reaction, forward_guess, adjoint_guess, observed):
        rows, cols = control.shape
        grid_rows = rows * X
        tiles = (grid_rows // SUB) * (cols // LANES)
        own_tiles = (rows // SUB) * (cols // LANES)
        vmem = pl.BlockSpec(memory_space=pltpu.VMEM)
        f32 = lambda *shape: pltpu.VMEM(shape, jnp.float32)
        dma = lambda *shape: pltpu.SemaphoreType.DMA(shape)
        outs = pl.pallas_call(
            functools.partial(kernel, T, X),
            out_shape=(
                jax.ShapeDtypeStruct(forward_guess.shape, jnp.float32),
                jax.ShapeDtypeStruct(forward_guess.shape, jnp.float32),
                jax.ShapeDtypeStruct(control.shape, jnp.float32),
            ),
            in_specs=[pl.BlockSpec(memory_space=pl.ANY)] * 7,
            out_specs=(vmem,) * 3,
            scratch_shapes=[
                f32(SLOTS, grid_rows, cols),
                f32(rows, cols),
                f32(grid_rows, cols),
                f32(grid_rows, cols),
                f32(COARSEN - 1, grid_rows, cols),
                f32(grid_rows, cols),
                f32(SUMS, grid_rows, cols),
                f32(T, SUB, LANES),
                f32(T, SUB, LANES),
                f32(T, SUB, LANES),
                f32(T, SUB, LANES),
                f32(T, 2, SUB, LANES),
                f32(SUMS, SUB, LANES),
                f32(rows, cols),
                f32(2, rows, cols),
                dma(8),
                pltpu.SemaphoreType.REGULAR(((T - 2).bit_length(),)),
                dma(SLOTS, X), dma(SLOTS, X),
                dma(tiles), dma(T), dma(tiles), dma(T), dma(tiles), dma(T),
                dma(T), dma(tiles), dma(T), dma(tiles), dma(T), dma(tiles),
                dma(T), dma(own_tiles), dma(T), dma(own_tiles),
            ],
            compiler_params=pltpu.CompilerParams(collective_id=0, has_side_effects=True),
        )(control, initial, diffusion, reaction, forward_guess, adjoint_guess, observed)
        return pl.pallas_call(
            emit,
            out_shape=tuple(jax.ShapeDtypeStruct(out.shape, out.dtype) for out in outs),
            in_specs=[vmem] * 3,
            out_specs=(vmem,) * 3,
        )(*outs)

    return jax.shard_map(
        shards,
        mesh=mesh,
        in_specs=(
            P("space", None),
            P("space", None),
            P("space", None),
            P("space", None),
            P("tm", "space", None),
            P("tm", "space", None),
            P("tm", "space", None),
        ),
        out_specs=(P("tm", "space", None), P("tm", "space", None), P("space", None)),
        check_vma=False,
    )
```

time: 38.6 us -> 34.3 us (0.89); the launches traced: 37.9 us -> 34.1 us
  local copies, waits for them, and re-layouts: 2.77 us -> 0 us
  Pallas kernels: 34.5 us -> 33.4 us
    unnamed x7 -> x0, local copies, waits for them, and re-layouts: 2.77 us -> none
    pallas_call x1, Pallas kernels: 34.5 us -> 32 us  [shards(): pl.pallas_call(functools.partial(kernel, T, X), out_shape=(jax.ShapeDtype...]
    pallas_call x0 -> x1, Pallas kernels: none -> 1.43 us  [shards(): pl.pallas_call(emit, out_shape=tuple((jax.ShapeDtypeStruct(out.shape, out...]
where the time goes in v2:
time: 34.3 us; the launch traced here: 34.1 us
  Pallas kernels  33.4 us (97%)
  between operations  0.64 us (2%)
    pallas_call x1, Pallas kernels, shards(): pl.pallas_call(functools.partial(kernel, T, X), out_shape=(jax.ShapeDtype...  32 us
    pallas_call x1, Pallas kernels, shards(): pl.pallas_call(emit, out_shape=tuple((jax.ShapeDtypeStruct(out.shape, out...  1.43 us

profile of v2, /device:TPU:0, one launch (start us, length us, event | category | flops | bytes accessed | tf_op | source)
XLA Modules:
  0.0 34.1 jit_solution(5947752149563281598)
XLA Ops:
  0.6 32.0 %shard_map.94 = (f32[1,16,512]{2,1,0:T(8,128)}, f32[1,16,512]{2,1,0:T(8,128)}, f32[16,512]{1,0:T(8,128)}) custom-call(f32[16,512]{1,0:T(8,128)} %control_ref.1, f32[16,512]{1,0:T(8,128)} %initial_ref.1, f32[16,512]{1,0:T(8,128)} %diffusion_ref.1, f32[16,512]{1,0:T(8,128)} %reaction_ref.1, f32[1,16,512]{2,1,0:T(8,128)} %guess_ref.1, ...), custom_call_target="tpu_custom_call" | custom-call | tf_op jit(solution)/shard_map/pallas_call | solution.py:521
  32.6 1.4 %shard_map.95 = (f32[1,16,512]{2,1,0:T(8,128)}, f32[1,16,512]{2,1,0:T(8,128)}, f32[16,512]{1,0:T(8,128)}) custom-call(f32[1,16,512]{2,1,0:T(8,128)} %get-tuple-element.6.refs_0_, f32[1,16,512]{2,1,0:T(8,128)} %get-tuple-element.7.refs_1_, f32[16,512]{1,0:T(8,128)} %get-tuple-element.8.refs_2_), custom_call_target="tpu_custom_call" | custom-call | tf_op jit(solution)/shard_map/pallas_call | solution.py:555

commit v3 on v2

--- a/solution.py
+++ b/solution.py
@@ -24,8 +24,8 @@
     states_out, adjoints_out, gradient_out,
     full, own_adjoint, weight, inverse, points, total, sums,
     gathered_target, gathered, gathered_adj, solved, solved_adj, packed, landed, landed_adj,
-    local_sem, reach, in_send, in_recv, m0_send, m0_recv, m1_send, m1_recv, m2_send, m2_recv,
-    b0_send, b0_recv, b1_send, b1_recv, b2_send, b2_recv, p1_send, p1_recv, p2_send, p2_recv,
+    local_sem, reach, in_send, in_recv, m0, m1, m2,
+    b0, b1, b2, p1, p2,
 ):
     rows, cols = control_ref.shape
     grid_rows = rows * X
@@ -247,93 +247,109 @@
     owner = jnp.logical_and(lax.rem(j, stride) == 0, mine < tiles)
     my_rows, my_cols = tile_rows(lax.rem(mine, tiles)), tile_cols(lax.rem(mine, tiles))
 
-    def scatter(act, slot, target, send_sem, recv_sem):
-        def body(i, c):
-            d = lax.rem(mine + i, tiles)
-
-            @pl.when(d * stride != j)
-            def _():
-                act(pltpu.make_async_remote_copy(
-                    src_ref=full.at[slot, tile_rows(d), tile_cols(d)], dst_ref=target.at[j],
-                    send_sem=send_sem.at[d], recv_sem=recv_sem.at[j],
-                    device_id=device(d * stride, x), device_id_type=MESH,
-                ))
-
-            return c
-
-        lax.fori_loop(0, tiles, body, 0)
-
-    def await_gather(slot, target, send_sem, recv_sem):
+    ordered = T & (T - 1) == 0 and T <= 32
+    flips = [(1 << n, (1 << n) * (1 - 2 * lax.rem(j // (1 << n), 2))) for n in range((T - 1).bit_length())]
+
+    def each_other(f):
+        if ordered:
+            for i in range(T - 1, 0, -1):
+                f(sum(flip for bit, flip in flips if i & bit) + j)
+        else:
+            def body(i, c):
+                f(lax.rem(j + i, T))
+                return c
+
+            lax.fori_loop(1, T, body, 0)
+
+    every_owner = tiles == T
+
+    def each_owner(f):
+        if every_owner:
+            each_other(f)
+        else:
+            def body(i, c):
+                d = lax.rem(mine + i, tiles)
+
+                @pl.when(d * stride != j)
+                def _():
+                    f(d)
+
+                return c
+
+            lax.fori_loop(0, tiles, body, 0)
+
+    def drained(buffer, sems, count, less, receive):
+        def wait(n):
+            ref = buffer.at[pl.ds(0, n)]
+            copy = pltpu.make_async_remote_copy(
+                src_ref=ref, dst_ref=ref, send_sem=sems.at[0], recv_sem=sems.at[1],
+                device_id=device(lax.rem(j + 1, T), x), device_id_type=MESH,
+            )
+            if receive:
+                copy.wait_recv()
+            else:
+                copy.wait_send()
+
+        if less is True:
+            wait(count - 1)
+        else:
+            pl.when(less)(lambda: wait(count - 1))
+            pl.when(jnp.logical_not(less))(lambda: wait(count))
+
+    is_owner = True if every_owner else owner
+
+    def scatter(slot, target, sems):
+        def one(d):
+            pltpu.make_async_remote_copy(
+                src_ref=full.at[slot, tile_rows(d), tile_cols(d)], dst_ref=target.at[j],
+                send_sem=sems.at[0], recv_sem=sems.at[1],
+                device_id=device(d * stride, x), device_id_type=MESH,
+            ).start()
+
+        each_owner(one)
+
+    def scattered(target, sems):
+        drained(target, sems, tiles, is_owner, False)
+
+    def await_gather(slot, target, sems):
         target[j] = full[slot, my_rows, my_cols]
-
-        def body(i, c):
-            k = lax.rem(j + i, T)
+        drained(target, sems, T, True, True)
+
+    def spread_sums(slot, sems):
+        def one(k):
             pltpu.make_async_remote_copy(
-                src_ref=full.at[slot, my_rows, my_cols], dst_ref=target.at[k],
-                send_sem=send_sem.at[0], recv_sem=recv_sem.at[k],
+                src_ref=packed.at[slot], dst_ref=sums.at[slot, my_rows, my_cols],
+                send_sem=sems.at[0], recv_sem=sems.at[1],
                 device_id=device(k, x), device_id_type=MESH,
-            ).wait_recv()
-            return c
-
-        lax.fori_loop(1, T, body, 0)
-
-    def spread_sums(act, slot, send_sem, recv_sem):
-        def body(i, c):
-            k = lax.rem(j + i, T)
-            act(pltpu.make_async_remote_copy(
-                src_ref=packed.at[slot], dst_ref=sums.at[slot, my_rows, my_cols],
-                send_sem=send_sem.at[k], recv_sem=recv_sem.at[mine],
-                device_id=device(k, x), device_id_type=MESH,
-            ))
-            return c
-
-        lax.fori_loop(1, T, body, 0)
-
-    def await_sums(slot, send_sem, recv_sem):
-        def body(d, c):
-            @pl.when(d * stride != j)
-            def _():
-                pltpu.make_async_remote_copy(
-                    src_ref=packed.at[slot], dst_ref=sums.at[slot, tile_rows(d), tile_cols(d)],
-                    send_sem=send_sem.at[0], recv_sem=recv_sem.at[d],
-                    device_id=device(d * stride, x), device_id_type=MESH,
-                ).wait_recv()
-
-            return c
-
-        lax.fori_loop(0, tiles, body, 0)
+            ).start()
+
+        each_other(one)
+
+    def sums_spread(sems):
+        drained(gathered, sems, T, True, False)
+
+    def await_sums(sems):
+        drained(gathered, sems, tiles, is_owner, True)
 
     local = mine - x * own_tiles
     holds_output = jnp.logical_and(owner, jnp.logical_and(local >= 0, local < own_tiles))
     local_tile = lax.rem(local + tiles, own_tiles)
 
-    def spread_solved(act, source, landing, send_sem, recv_sem):
-        def body(i, c):
-            k = lax.rem(j + i, T)
-            act(pltpu.make_async_remote_copy(
+    def spread_solved(source, landing, sems):
+        def one(k):
+            pltpu.make_async_remote_copy(
                 src_ref=source.at[k], dst_ref=landing(local_tile),
-                send_sem=send_sem.at[k], recv_sem=recv_sem.at[local_tile],
+                send_sem=sems.at[0], recv_sem=sems.at[1],
                 device_id=device(k, x), device_id_type=MESH,
-            ))
-            return c
-
-        lax.fori_loop(1, T, body, 0)
-
-    def await_solved(source, landing, send_sem, recv_sem):
-        def body(d, c):
-            source_tm = (d + x * own_tiles) * stride
-
-            @pl.when(source_tm != j)
-            def _():
-                pltpu.make_async_remote_copy(
-                    src_ref=source.at[0], dst_ref=landing(d),
-                    send_sem=send_sem.at[0], recv_sem=recv_sem.at[d],
-                    device_id=device(source_tm, x), device_id_type=MESH,
-                ).wait_recv()
-
-            return c
-
-        lax.fori_loop(0, own_tiles, body, 0)
+            ).start()
+
+        each_other(one)
+
+    def solved_spread(source, sems):
+        drained(source, sems, T, True, False)
+
+    def await_solved(source, sems):
+        drained(source, sems, own_tiles, holds_output, True)
 
     def landing(d):
         return landed.at[tile_rows(d), tile_cols(d)]
@@ -341,8 +357,6 @@
     def landing_adj(d):
         return landed_adj.at[:, tile_rows(d), tile_cols(d)]
 
-    start = lambda copy: copy.start()
-    finish = lambda copy: copy.wait_send()
 
     def forward_points(start, scale, beside=None):
         def body(i, v):
@@ -382,13 +396,13 @@
                 reached(rounds - 1)
             for o in range(1, X):
                 await_input(TARGET, o)
-            scatter(start, TARGET, gathered_target, m0_send, m0_recv)
+            scatter(TARGET, gathered_target, m0)
 
     v = forward_points(get(full, ENTRY), 1.0, beside_forward)
     v = forward_step(v, 1.0)
     keep = (j > 0).astype(jnp.float32)
     put(full, zipped(lambda a, d, s: a - keep * (d * s), v, cut(damping), get(full, ENTRY)), FORWARD)
-    scatter(start, FORWARD, gathered, m1_send, m1_recv)
+    scatter(FORWARD, gathered, m1)
 
     for o in range(1, X):
         await_input(GUESS, o)
@@ -409,22 +423,22 @@
     g = adjoint_step(misfit_added(get(full, EXIT), get(full, GUESS), get(full, TARGET)))
     g = lax.fori_loop(0, COARSEN - 1, adjoint_points(g, (full, TARGET)), g)
     put(full, zipped(lambda a, d, t: a - d * t, g, cut(damping), get(full, EXIT)), ADJOINT)
-    scatter(start, ADJOINT, gathered_adj, m2_send, m2_recv)
+    scatter(ADJOINT, gathered_adj, m2)
 
     @pl.when(owner)
     def _():
-        def share(slot, value, send_sem, recv_sem):
+        def share(slot, value, sems):
             packed[slot] = value
             sums[slot, my_rows, my_cols] = value
-            spread_sums(start, slot, send_sem, recv_sem)
+            spread_sums(slot, sems)
 
         my_damping = 1.0 / (1.0 + COARSEN * full[REACTION, my_rows, my_cols])
 
-        await_gather(TARGET, gathered_target, m0_send, m0_recv)
+        await_gather(TARGET, gathered_target, m0)
         target = lax.fori_loop(1, T, lambda k, c: c + gathered_target[k], gathered_target[0])
-        share(SUM_TARGET, target, b0_send, b0_recv)
-
-        await_gather(FORWARD, gathered, m1_send, m1_recv)
+        share(SUM_TARGET, target, b0)
+
+        await_gather(FORWARD, gathered, m1)
 
         def forward_body(k, carry):
             state, before, through = carry
@@ -435,9 +449,9 @@
         head = gathered[0]
         solved[0] = head
         _, before, states = lax.fori_loop(1, T, forward_body, (head,) * 3)
-        share(SUM_ENTRY, before, b1_send, b1_recv)
-
-        await_gather(ADJOINT, gathered_adj, m2_send, m2_recv)
+        share(SUM_ENTRY, before, b1)
+
+        await_gather(ADJOINT, gathered_adj, m2)
 
         def adjoint_body(i, carry):
             k = T - 1 - i
@@ -449,7 +463,7 @@
         head = gathered_adj[T - 1]
         solved_adj[T - 1, 0] = head
         _, before, adjoints = lax.fori_loop(1, T, adjoint_body, (head,) * 3)
-        share(SUM_EXIT, before + (states - target) * (1.0 / COARSEN), b2_send, b2_recv)
+        share(SUM_EXIT, before + (states - target) * (1.0 / COARSEN), b2)
 
         def fill(k, c):
             solved_adj[k, 1] = adjoints
@@ -459,17 +473,27 @@
 
     @pl.when(holds_output)
     def _():
-        spread_solved(start, solved_adj, landing_adj, p2_send, p2_recv)
-        spread_solved(start, solved, landing, p1_send, p1_recv)
+        spread_solved(solved_adj, landing_adj, p2)
+        spread_solved(solved, landing, p1)
         landed_adj[:, tile_rows(local_tile), tile_cols(local_tile)] = solved_adj[j]
         landed[tile_rows(local_tile), tile_cols(local_tile)] = solved[j]
 
-    await_sums(SUM_ENTRY, b1_send, b1_recv)
+    await_sums(b1)
     entry_sum = zipped(lambda a, c: a + c, get(sums, SUM_ENTRY), get(full, INITIAL))
     forward_points(entry_sum, float(T))
 
-    await_sums(SUM_TARGET, b0_send, b0_recv)
-    await_sums(SUM_EXIT, b2_send, b2_recv)
+    await_sums(b0)
+    input_sends(lambda copy: copy.wait_send())
+    scattered(gathered_target, m0)
+    scattered(gathered, m1)
+    scattered(gathered_adj, m2)
+
+    @pl.when(owner)
+    def _():
+        sums_spread(b0)
+        sums_spread(b1)
+
+    await_sums(b2)
     g = adjoint_step(get(sums, SUM_EXIT))
     put(total, g)
 
@@ -479,27 +503,18 @@
         return g
 
     lax.fori_loop(0, COARSEN - 2, final_body, g)
-    await_solved(solved_adj, landing_adj, p2_send, p2_recv)
+    await_solved(solved_adj, p2)
     gradient_out[...] = (landed_adj[1] + total[own, :]) * (1.0 / (COARSEN * T))
     adjoints_out[0] = landed_adj[0]
-    await_solved(solved, landing, p1_send, p1_recv)
+    await_solved(solved, p1)
     states_out[0] = landed[...]
 
-    input_sends(finish)
-    scatter(finish, TARGET, gathered_target, m0_send, m0_recv)
-    scatter(finish, FORWARD, gathered, m1_send, m1_recv)
-    scatter(finish, ADJOINT, gathered_adj, m2_send, m2_recv)
-
-    @pl.when(owner)
-    def _():
-        spread_sums(finish, SUM_TARGET, b0_send, b0_recv)
-        spread_sums(finish, SUM_ENTRY, b1_send, b1_recv)
-        spread_sums(finish, SUM_EXIT, b2_send, b2_recv)
+    pl.when(owner)(lambda: sums_spread(b2))
 
     @pl.when(holds_output)
     def _():
-        spread_solved(finish, solved_adj, landing_adj, p2_send, p2_recv)
-        spread_solved(finish, solved, landing, p1_send, p1_recv)
+        solved_spread(solved_adj, p2)
+        solved_spread(solved, p1)
 
 
 def emit(*refs):
@@ -546,9 +561,7 @@
                 dma(8),
                 pltpu.SemaphoreType.REGULAR(((T - 2).bit_length(),)),
                 dma(SLOTS, X), dma(SLOTS, X),
-                dma(tiles), dma(T), dma(tiles), dma(T), dma(tiles), dma(T),
-                dma(T), dma(tiles), dma(T), dma(tiles), dma(T), dma(tiles),
-                dma(T), dma(own_tiles), dma(T), dma(own_tiles),
+                *[dma(2)] * 8,
             ],
             compiler_params=pltpu.CompilerParams(collective_id=0, has_side_effects=True),
         )(control, initial, diffusion, reaction, forward_guess, adjoint_guess, observed)

time: 34.3 us -> 31.1 us (0.907)
  Pallas kernels: 33.4 us -> 30.2 us
    pallas_call x1, Pallas kernels: 32 us -> 28.8 us  [shards(): pl.pallas_call(functools.partial(kernel, T, X), out_shape=(jax.ShapeDtype...]
where the time goes in v3:
time: 31.1 us; the launch traced here: 30.8 us
  Pallas kernels  30.2 us (97%)
  between operations  0.64 us (2%)
    pallas_call x1, Pallas kernels, shards(): pl.pallas_call(functools.partial(kernel, T, X), out_shape=(jax.ShapeDtype...  28.8 us
    pallas_call x1, Pallas kernels, shards(): pl.pallas_call(emit, out_shape=tuple((jax.ShapeDtypeStruct(out.shape, out...  1.43 us

profile of v3, /device:TPU:0, one launch (start us, length us, event | category | flops | bytes accessed | tf_op | source)
XLA Modules:
  0.0 30.8 jit_solution(1799260109630361371)
XLA Ops:
  0.6 28.8 %shard_map.94 = (f32[1,16,512]{2,1,0:T(8,128)}, f32[1,16,512]{2,1,0:T(8,128)}, f32[16,512]{1,0:T(8,128)}) custom-call(f32[16,512]{1,0:T(8,128)} %control_ref.1, f32[16,512]{1,0:T(8,128)} %initial_ref.1, f32[16,512]{1,0:T(8,128)} %diffusion_ref.1, f32[16,512]{1,0:T(8,128)} %reaction_ref.1, f32[1,16,512]{2,1,0:T(8,128)} %guess_ref.1, ...), custom_call_target="tpu_custom_call" | custom-call | tf_op jit(solution)/shard_map/pallas_call | solution.py:536
  29.4 1.4 %shard_map.95 = (f32[1,16,512]{2,1,0:T(8,128)}, f32[1,16,512]{2,1,0:T(8,128)}, f32[16,512]{1,0:T(8,128)}) custom-call(f32[1,16,512]{2,1,0:T(8,128)} %get-tuple-element.6.refs_0_, f32[1,16,512]{2,1,0:T(8,128)} %get-tuple-element.7.refs_1_, f32[16,512]{1,0:T(8,128)} %get-tuple-element.8.refs_2_), custom_call_target="tpu_custom_call" | custom-call | tf_op jit(solution)/shard_map/pallas_call | solution.py:568
